TPU v7x, 128 devices: a whole 4x4x4 slice. The times are simulated.
128 devices in a mesh: rep: 2 (over core), dp: 64 (over x, y, z).
Axes of the slice: x: 4, y: 4, z: 4, core: 2. Of those that a mesh axis runs over, the one named last changes fastest.
Arguments:
- x: bfloat16 [128, 2048, 1280], P(('rep', 'dp')), parts along dimension 0
- dy: bfloat16 [128, 2048, 1280], P(('rep', 'dp')), parts along dimension 0
- w_gate: bfloat16 [2, 1280, 3072], replicated
- w_up: bfloat16 [2, 1280, 3072], replicated
- w_down: bfloat16 [2, 3072, 1280], replicated
- m_w_gate: float32 [2, 1280, 3072], P(None, 'dp')
- m_w_up: float32 [2, 1280, 3072], P(None, 'dp')
- m_w_down: float32 [2, 3072, 1280], P(None, 'dp')
- v_w_gate: float32 [2, 1280, 3072], P(None, 'dp')
- v_w_up: float32 [2, 1280, 3072], P(None, 'dp')
- v_w_down: float32 [2, 3072, 1280], P(None, 'dp')
Outputs:
- output 1: bfloat16 [4, 1280, 3072], P('rep'), parts along dimension 0
- output 2: bfloat16 [4, 1280, 3072], P('rep'), parts along dimension 0
- output 3: bfloat16 [4, 3072, 1280], P('rep'), parts along dimension 0
- output 4: float32 [4, 1280, 3072], P('rep', 'dp'), parts along dimension 0
- output 5: float32 [4, 1280, 3072], P('rep', 'dp'), parts along dimension 0
- output 6: float32 [4, 3072, 1280], P('rep', 'dp'), parts along dimension 0
- output 7: float32 [4, 1280, 3072], P('rep', 'dp'), parts along dimension 0
- output 8: float32 [4, 1280, 3072], P('rep', 'dp'), parts along dimension 0
- output 9: float32 [4, 3072, 1280], P('rep', 'dp'), parts along dimension 0
There are 2 independent parts. A program takes and returns all parts, laid end to end along the dimension named above; an argument that names none is the same for every part.
All inputs are finite; a program needn't handle non-finite values.
Results may differ from a plain program's by a relative error of at most 0.022.
Values are sent between devices in bfloat16 or wider.
A program may use at most 1.5 GiB of HBM per device.

v0:
```python
import jax
import jax.numpy as jnp
from jax import lax

NAMES = ("w_gate", "w_up", "w_down")


def matmul(a, w):
    return jnp.dot(a, w, preferred_element_type=jnp.float32).astype(jnp.bfloat16)


def normed(h):
    wide = h.astype(jnp.float32)
    scale = lax.rsqrt(jnp.mean(wide**2, -1, keepdims=True) + 1e-6)
    return (wide * scale).astype(jnp.bfloat16)


def layer(h, w):
    a = normed(h)
    gate = jnp.dot(a, w["w_gate"], preferred_element_type=jnp.float32)
    up = jnp.dot(a, w["w_up"], preferred_element_type=jnp.float32)
    return h + matmul((jax.nn.silu(gate) * up).astype(jnp.bfloat16), w["w_down"])


def adamw(w, m, v, g):
    m = 0.9 * m + 0.1 * g
    v = 0.95 * v + 0.05 * g * g
    step = m * lax.rsqrt(v + 1e-8) + 0.1 * w
    return (w - 0.02 * step).astype(jnp.bfloat16), m, v


def clipped(gradients, sum_of_squares, count):
    factor = jnp.minimum(1.0, 0.5 * lax.rsqrt(sum_of_squares / count + 1e-30))
    return [g * factor for g in gradients]


def stack(weights, h):
    for number in range(weights["w_gate"].shape[0]):
        h = layer(h, {name: w[number] for name, w in weights.items()})
    return h


def solution(mesh):
    groups = mesh.shape["rep"]

    def step(x, dy, *arrays):
        weights, m, v = (arrays[i : i + 3] for i in (0, 3, 6))
        x, dy = (t.reshape(groups, -1, *t.shape[1:]) for t in (x, dy))

        def of_a_group(x, dy):
            _, back = jax.vjp(lambda w: stack(w, x), dict(zip(NAMES, weights, strict=True)))
            by_weights = back(dy)[0]
            gradients = [by_weights[name].astype(jnp.float32) for name in NAMES]
            gradients = clipped(gradients, sum(jnp.sum(g * g) for g in gradients), sum(g.size for g in gradients))
            new = [adamw(w.astype(jnp.float32), m, v, g) for w, m, v, g in zip(weights, m, v, gradients, strict=True)]
            return tuple(one[which] for which in range(3) for one in new)

        return tuple(t.reshape(-1, *t.shape[2:]) for t in jax.vmap(of_a_group)(x, dy))

    return step
```

profile of v0, /device:TPU:0, one launch (start us, length us, event | category | flops | bytes accessed | tf_op | source)
XLA Modules:
  0.0 2142.8 jit_solution(9281761091007830740)
XLA Ops:
  10.8 7.9 copy.11
  18.8 20.3 fusion.67
  39.1 28.4 %fusion.65 = f32[2048,3072]{1,0:T(8,128)} fusion(bf16[2,1280,3072]{2,1,0:T(8,128)(2,1)} %param.3, bf16[1,2048,1280]{2,1,0:T(8,128)(2,1)} %param.2, f32[2048]{0:T(1024)S(1)} %add_rsqrt_fusion), kind=kOutput, calls=%fused_computation.76 | convolution fusion | flops 16113991680 | bytes 38281216 | tf_op jit(solution)/vmap(jvp())/dot_general | solution.py:21
  67.5 16.4 fusion.39
  83.9 22.7 %fusion.51 = (f32[2048]{0:T(1024)S(1)}, bf16[1,1,2048,1280]{2,3,1,0:T(8,128)(2,1)S(1)}) fusion(bf16[2048,3072]{1,0:T(8,128)(2,1)} %fusion.39, bf16[2,3072,1280]{2,1,0:T(8,128)(2,1)} %param.4, bf16[1,2048,1280]{1,2,0:T(8,128)(2,1)} %copy.11), kind=kOutput, calls=%fused_computation.61 | convolution fusion | flops 16119232512 | bytes 30941184 | tf_op jit(solution)/vmap(jvp())/dot_general | solution.py:9
  107.3 23.2 %fusion.56 = f32[2048,3072]{1,0:T(8,128)} fusion(bf16[2,1280,3072]{2,1,0:T(8,128)(2,1)} %param, bf16[1,1,2048,1280]{2,3,1,0:T(8,128)(2,1)S(1)} %get-tuple-element.78, f32[2048]{0:T(1024)S(1)} %bitcast.385), kind=kOutput, calls=%fused_computation.67 | convolution fusion | flops 16113991680 | bytes 38281216 | tf_op jit(solution)/vmap(jvp())/dot_general | solution.py:20
  130.5 22.3 %fusion.59 = f32[2048,3072]{1,0:T(8,128)} fusion(bf16[2,1280,3072]{2,1,0:T(8,128)(2,1)} %param.3, bf16[1,1,2048,1280]{2,3,1,0:T(8,128)(2,1)S(1)} %get-tuple-element.78, f32[2048]{0:T(1024)S(1)} %bitcast.386), kind=kOutput, calls=%fused_computation.70 | convolution fusion | flops 16113991680 | bytes 38281216 | tf_op jit(solution)/vmap(jvp())/dot_general | solution.py:21
  152.7 22.0 %convolution_convert_fusion.1 = bf16[2048,3072]{1,0:T(8,128)(2,1)} fusion(bf16[2,3072,1280]{2,1,0:T(8,128)(2,1)} %param.4, bf16[1,2048,1280]{2,1,0:T(8,128)(2,1)S(1)} %bitcast.379), kind=kOutput, calls=%fused_computation.56 | convolution fusion | flops 16112418816 | bytes 25690112 | tf_op jit(solution)/vmap(transpose(jvp()))/dot_general | solution.py:9
  174.7 7.9 copy.12
  182.6 24.5 %fusion.78 = bf16[2048,1280]{0,1:T(8,128)(2,1)} fusion(bf16[2048,3072]{1,0:T(8,128)(2,1)} %convolution_convert_fusion.1, f32[2048,3072]{1,0:T(8,128)} %fusion.56, bf16[2,1280,3072]{2,1,0:T(8,128)(2,1)} %param.3), kind=kOutput, calls=%fused_computation.85 | convolution fusion | flops 16146497536 | bytes 50855936 | tf_op jit(solution)/vmap(transpose(jvp()))/dot_general | solution.py:21
  207.1 21.2 fusion.10
  228.4 25.0 %fusion.53 = (f32[2048]{0:T(1024)S(1)}, bf16[1,1,2048,1280]{2,3,1,0:T(8,128)(2,1)}) fusion(bf16[1,1,2048,1280]{2,3,1,0:T(8,128)(2,1)} %copy-done.3, bf16[2048,1280]{0,1:T(8,128)(2,1)} %fusion.78, bf16[2048,3072]{1,0:T(8,128)(2,1)S(1)} %fusion.10, bf16[2,1280,3072]{2,1,0:T(8,128)(2,1)} %param), kind=kOutput, calls=%fused_computation.63 | convolution fusion | flops 16119232512 | bytes 36184064 | tf_op jit(solution)/vmap(transpose(jvp()))/dot_general | solution.py:20
  253.5 12.4 fusion.104
  265.9 22.5 %convolution_bitcast_fusion = f32[1,3072,1280]{2,1,0:T(8,128)} fusion(bf16[2048,3072]{1,0:T(8,128)(2,1)} %fusion.39, bf16[2048,1280]{0,1:T(8,128)(2,1)} %fusion.104), kind=kOutput, calls=%fused_computation.45 | convolution fusion | flops 16106127360 | bytes 33554432 | tf_op jit(solution)/vmap(transpose(jvp()))/dot_general | solution.py:9
  288.5 23.0 %convolution_convert_fusion = bf16[2048,3072]{1,0:T(8,128)(2,1)} fusion(bf16[2048,1280]{0,1:T(8,128)(2,1)} %fusion.104, bf16[2,3072,1280]{2,1,0:T(8,128)(2,1)} %param.4), kind=kOutput, calls=%fused_computation.55 | convolution fusion | flops 16112418816 | bytes 25690112 | tf_op jit(solution)/vmap(transpose(jvp()))/dot_general | solution.py:9
  311.5 26.6 %fusion.30 = f32[1,1280,3072]{2,1,0:T(8,128)} fusion(bf16[2048,3072]{1,0:T(8,128)(2,1)} %convolution_convert_fusion.1, f32[2048,3072]{1,0:T(8,128)} %fusion.56, bf16[1,1,2048,1280]{2,3,1,0:T(8,128)(2,1)} %copy-done.3, f32[2048]{0:T(1024)S(1)} %bitcast.388), kind=kOutput, calls=%fused_computation.42 | convolution fusion | flops 16151740416 | bytes 58728448 | tf_op jit(solution)/vmap(transpose(jvp()))/dot_general | solution.py:21
  338.2 25.4 %fusion.36 = f32[1,1280,3072]{2,1,0:T(8,128)} fusion(bf16[2048,3072]{1,0:T(8,128)(2,1)} %convolution_convert_fusion, f32[2048,3072]{1,0:T(8,128)} %copy-done, bf16[1,2048,1280]{1,2,0:T(8,128)(2,1)S(1)} %bitcast.381, f32[2048]{0:T(1024)S(1)} %copy-done.23), kind=kOutput, calls=%fused_computation.44 | convolution fusion | flops 16151740416 | bytes 58728448 | tf_op jit(solution)/vmap(transpose(jvp()))/dot_general | solution.py:21
  363.6 441.8 %fusion.159 = (f32[24,3072]{1,0:T(8,128)S(1)}, f32[24,3072]{1,0:T(8,128)S(1)}) fusion(f32[1,1280,3072]{2,1,0:T(8,128)} %fusion.36, f32[1,1280,3072]{2,1,0:T(8,128)} %fusion.30), kind=kCustom, calls=%all-reduce-scatter.5 | all-reduce-scatter fusion | flops 9437185 | bytes 32047616
  811.0 31.0 %convolution_bitcast_fusion.1 = f32[1,3072,1280]{2,1,0:T(8,128)} fusion(f32[2048,3072]{1,0:T(8,128)} %fusion.59, f32[2048,3072]{1,0:T(8,128)} %fusion.56, bf16[1,2048,1280]{2,1,0:T(8,128)(2,1)} %param.5), kind=kOutput, calls=%fused_computation.46 | convolution fusion | flops 16143876096 | bytes 71303168 | tf_op jit(solution)/vmap(transpose(jvp()))/dot_general | solution.py:9
  842.0 22.7 %convolution_bitcast_fusion.2 = f32[1,1280,3072]{2,1,0:T(8,128)} fusion(bf16[2048,3072]{1,0:T(8,128)(2,1)} %copy-done.2, bf16[1,1,2048,1280]{2,3,1,0:T(8,128)(2,1)} %copy-done.3, f32[2048]{0:T(1024)S(1)} %bitcast.389), kind=kOutput, calls=%fused_computation.47 | convolution fusion | flops 16113991680 | bytes 33562624 | tf_op jit(solution)/vmap(transpose(jvp()))/dot_general | solution.py:20
  864.7 34.1 %fusion.33 = f32[1,1280,3072]{2,1,0:T(8,128)} fusion(f32[2048,3072]{1,0:T(8,128)} %copy-done, f32[2048,3072]{1,0:T(8,128)} %fusion.65, bf16[2048,3072]{1,0:T(8,128)(2,1)} %convolution_convert_fusion, bf16[1,2048,1280]{1,2,0:T(8,128)(2,1)} %copy.11, f32[2048]{0:T(1024)S(1)} %copy-done.23), kind=kOutput, calls=%fused_computation.43 | convolution fusion | flops 16183197696 | bytes 83894272 | tf_op jit(solution)/vmap(transpose(jvp()))/dot_general | solution.py:20
  898.8 447.2 %fusion.158 = (f32[24,3072]{1,0:T(8,128)S(1)}, f32[24,3072]{1,0:T(8,128)S(1)}) fusion(f32[1,1280,3072]{2,1,0:T(8,128)} %fusion.33, f32[1,1280,3072]{2,1,0:T(8,128)} %convolution_bitcast_fusion.2), kind=kCustom, calls=%all-reduce-scatter.4 | all-reduce-scatter fusion | flops 9437185 | bytes 32047616
  1507.6 17.5 concatenate.2
  1525.1 33.8 %concatenate.3 = bf16[276,3072]{1,0:T(8,128)(2,1)} concatenate(bf16[12,3072]{1,0:T(8,128)(2,1)} %collective-permute-done.43, bf16[24,3072]{1,0:T(8,128)(2,1)} %collective-permute-done.42, bf16[24,3072]{1,0:T(8,128)(2,1)} %collective-permute-done.41, bf16[24,3072]{1,0:T(8,128)(2,1)} %collective-permute-done.40, bf16[24,3072]{1,0:T(8,128)(2,1)} %collective-permute-done.39, ...), dimensions={0} | concatenate | bytes 3538944
  1558.9 33.8 %concatenate = bf16[276,3072]{1,0:T(8,128)(2,1)} concatenate(bf16[12,3072]{1,0:T(8,128)(2,1)} %collective-permute-done.10, bf16[24,3072]{1,0:T(8,128)(2,1)} %collective-permute-done.9, bf16[24,3072]{1,0:T(8,128)(2,1)} %collective-permute-done.8, bf16[24,3072]{1,0:T(8,128)(2,1)} %collective-permute-done.7, bf16[24,3072]{1,0:T(8,128)(2,1)} %collective-permute-done.6, ...), dimensions={0} | concatenate | bytes 3538944
  1592.8 33.8 %concatenate.1 = bf16[276,3072]{1,0:T(8,128)(2,1)} concatenate(bf16[12,3072]{1,0:T(8,128)(2,1)} %collective-permute-done.21, bf16[24,3072]{1,0:T(8,128)(2,1)} %collective-permute-done.20, bf16[24,3072]{1,0:T(8,128)(2,1)} %collective-permute-done.19, bf16[24,3072]{1,0:T(8,128)(2,1)} %collective-permute-done.18, bf16[24,3072]{1,0:T(8,128)(2,1)} %collective-permute-done.17, ...), dimensions={0} | concatenate | bytes 3538944
  1635.0 173.7 %all-reduce.10 = f32[1]{0:T(128)} all-reduce(f32[1]{0:T(128)} %bitcast.50), channel_id=3, replica_groups=mesh['rep'=2,'dp'=64] {'dp'}, use_global_device_ids=true, to_apply=%region_3.4.clone | all-reduce | flops 1 | bytes 8 | tf_op jit(solution)/vmap()/reduce_sum | solution.py:54
  1822.3 84.6 %all-gather.14.cloned.1.call-done = bf16[1,2,3072,1280]{3,2,1,0:T(8,128)(2,1)} async-done(((bf16[1,2,48,1280]{3,2,1,0:T(8,128)(2,1)}), bf16[1,2,3072,1280]{3,2,1,0:T(8,128)(2,1)}) %all-gather.14.cloned.1.call-update) | async-done | bytes 15728656 | tf_op jit(solution)/reshape | solution.py:58
  1906.8 103.3 %all-gather.12.cloned.1.call-done = bf16[1,2,1280,3072]{3,1,0,2:T(2,128)(2,1)} async-done(((bf16[1,2,20,3072]{3,1,0,2:T(2,128)(2,1)}), bf16[1,2,1280,3072]{3,1,0,2:T(2,128)(2,1)}) %all-gather.12.cloned.1.call-update) | async-done | bytes 15728656 | tf_op jit(solution)/reshape | solution.py:58
  2010.1 15.5 copy.19
  2025.6 87.8 %all-gather.10.cloned.1.call-done = bf16[1,2,1280,3072]{3,1,0,2:T(2,128)(2,1)} async-done(((bf16[1,2,20,3072]{3,1,0,2:T(2,128)(2,1)}), bf16[1,2,1280,3072]{3,1,0,2:T(2,128)(2,1)}) %all-gather.10.cloned.1.call-update) | async-done | bytes 15728656 | tf_op jit(solution)/reshape | solution.py:58
  2113.4 16.6 copy.18
  (192 shorter events, 195.1 us)
Async XLA Ops:
  7.2 1624.5 %reduce-scatter.25.cloned.1.call-start = ((), (), s32[]{:S(2)}) async-start(), calls=%async_computation.6 | async-start | bytes 15974400
  288.4 1344.3 %reduce-scatter.23.cloned.1.call-start = ((), (), s32[]{:S(2)}) async-start(), calls=%async_computation.5 | async-start | bytes 15974400
  806.1 547.2 %collective-permute-start.32 = (bf16[12,3072]{1,0:T(8,128)(2,1)}, bf16[12,3072]{1,0:T(8,128)(2,1)}, u32[]{:S(2)}, u32[]{:S(2)}) collective-permute-start(bf16[12,3072]{1,0:T(8,128)(2,1)} %slice.26), channel_id=1, source_target_pairs={{0,11},{1,12},{2,13},{3,14},{4,15},{5,16},{6,17},{7,18},{8,19},{9,... | collective-permute-start | bytes 221192
  808.7 548.2 %collective-permute-start.43 = (bf16[12,3072]{1,0:T(8,128)(2,1)}, bf16[12,3072]{1,0:T(8,128)(2,1)}, u32[]{:S(2)}, u32[]{:S(2)}) collective-permute-start(bf16[12,3072]{1,0:T(8,128)(2,1)} %slice.27), channel_id=1, source_target_pairs={{0,11},{1,12},{2,13},{3,14},{4,15},{5,16},{6,17},{7,18},{8,19},{9,... | collective-permute-start | bytes 221192
  842.0 1064.9 %all-gather.14.cloned.1.call-start = ((), (), s32[]{:S(2)}) async-start(), calls=%async_computation.4 | async-start | bytes 15974400 | tf_op jit(solution)/reshape | solution.py:58
  1348.1 18.9 collective-permute-start.21
  1353.3 19.3 collective-permute-start.23
  1357.0 19.8 collective-permute-start.24
  1368.4 22.7 %collective-permute-start.27 = (bf16[24,3072]{1,0:T(8,128)(2,1)S(1)}, bf16[24,3072]{1,0:T(8,128)(2,1)S(1)}, u32[]{:S(2)}, u32[]{:S(2)}) collective-permute-start(bf16[24,3072]{1,0:T(8,128)(2,1)S(1)} %convert.122), channel_id=1, source_target_pairs={{0,6},{1,7},{2,8},{3,9},{4,10},{5,11},{6,12},{7,13},{8,14},{9,15},... | collective-permute-start | bytes 442376
  1372.7 19.8 collective-permute-start.28
  1376.8 22.4 %collective-permute-start.29 = (bf16[24,3072]{1,0:T(8,128)(2,1)S(1)}, bf16[24,3072]{1,0:T(8,128)(2,1)S(1)}, u32[]{:S(2)}, u32[]{:S(2)}) collective-permute-start(bf16[24,3072]{1,0:T(8,128)(2,1)S(1)} %convert.122), channel_id=1, source_target_pairs={{0,8},{1,9},{2,10},{3,11},{4,12},{5,13},{6,14},{7,15},{8,16},{9,17... | collective-permute-start | bytes 442376
  1380.6 20.6 collective-permute-start.30
  1384.0 24.7 %collective-permute-start.31 = (bf16[24,3072]{1,0:T(8,128)(2,1)S(1)}, bf16[24,3072]{1,0:T(8,128)(2,1)S(1)}, u32[]{:S(2)}, u32[]{:S(2)}) collective-permute-start(bf16[24,3072]{1,0:T(8,128)(2,1)S(1)} %convert.122), channel_id=1, source_target_pairs={{0,10},{1,11},{2,12},{3,13},{4,14},{5,15},{6,16},{7,17},{8,18},{9,... | collective-permute-start | bytes 442376
  1391.1 22.3 %collective-permute-start.33 = (bf16[24,3072]{1,0:T(8,128)(2,1)S(1)}, bf16[24,3072]{1,0:T(8,128)(2,1)S(1)}, u32[]{:S(2)}, u32[]{:S(2)}) collective-permute-start(bf16[24,3072]{1,0:T(8,128)(2,1)S(1)} %convert.123), channel_id=1, source_target_pairs={{0,1},{1,2},{2,3},{3,4},{4,5},{5,6},{6,7},{7,8},{8,9},{9,10},{10,1... | collective-permute-start | bytes 442376
  1392.4 24.4 %collective-permute-start.34 = (bf16[24,3072]{1,0:T(8,128)(2,1)S(1)}, bf16[24,3072]{1,0:T(8,128)(2,1)S(1)}, u32[]{:S(2)}, u32[]{:S(2)}) collective-permute-start(bf16[24,3072]{1,0:T(8,128)(2,1)S(1)} %convert.123), channel_id=1, source_target_pairs={{0,2},{1,3},{2,4},{3,5},{4,6},{5,7},{6,8},{7,9},{8,10},{9,11},{10,... | collective-permute-start | bytes 442376
  1399.2 24.6 %collective-permute-start.35 = (bf16[24,3072]{1,0:T(8,128)(2,1)S(1)}, bf16[24,3072]{1,0:T(8,128)(2,1)}, u32[]{:S(2)}, u32[]{:S(2)}) collective-permute-start(bf16[24,3072]{1,0:T(8,128)(2,1)S(1)} %convert.123), channel_id=1, source_target_pairs={{0,3},{1,4},{2,5},{3,6},{4,7},{5,8},{6,9},{7,10},{8,11},{9,12},{10... | collective-permute-start | bytes 442376
  1401.2 24.6 %collective-permute-start.36 = (bf16[24,3072]{1,0:T(8,128)(2,1)S(1)}, bf16[24,3072]{1,0:T(8,128)(2,1)}, u32[]{:S(2)}, u32[]{:S(2)}) collective-permute-start(bf16[24,3072]{1,0:T(8,128)(2,1)S(1)} %convert.123), channel_id=1, source_target_pairs={{0,4},{1,5},{2,6},{3,7},{4,8},{5,9},{6,10},{7,11},{8,12},{9,13},{1... | collective-permute-start | bytes 442376
  1408.7 19.0 collective-permute-start.37
  1413.4 19.3 collective-permute-start.38
  1441.2 20.9 collective-permute-start.3
  1445.9 18.8 collective-permute-start.4
  1448.5 22.7 %collective-permute-start.5 = (bf16[24,3072]{1,0:T(8,128)(2,1)S(1)}, bf16[24,3072]{1,0:T(8,128)(2,1)}, u32[]{:S(2)}, u32[]{:S(2)}) collective-permute-start(bf16[24,3072]{1,0:T(8,128)(2,1)S(1)} %convert.124), channel_id=1, source_target_pairs={{0,6},{1,7},{2,8},{3,9},{4,10},{5,11},{6,12},{7,13},{8,14},{9,15},... | collective-permute-start | bytes 442376
  1452.9 22.3 %collective-permute-start.6 = (bf16[24,3072]{1,0:T(8,128)(2,1)S(1)}, bf16[24,3072]{1,0:T(8,128)(2,1)}, u32[]{:S(2)}, u32[]{:S(2)}) collective-permute-start(bf16[24,3072]{1,0:T(8,128)(2,1)S(1)} %convert.124), channel_id=1, source_target_pairs={{0,7},{1,8},{2,9},{3,10},{4,11},{5,12},{6,13},{7,14},{8,15},{9,16}... | collective-permute-start | bytes 442376
  1456.7 21.3 collective-permute-start.7
  1464.7 19.3 collective-permute-start.9
  1486.5 106.2 %collective-permute-start.16 = (bf16[24,3072]{1,0:T(8,128)(2,1)}, bf16[24,3072]{1,0:T(8,128)(2,1)}, u32[]{:S(2)}, u32[]{:S(2)}) collective-permute-start(bf16[24,3072]{1,0:T(8,128)(2,1)} %convert.125), channel_id=1, source_target_pairs={{0,6},{1,7},{2,8},{3,9},{4,10},{5,11},{6,12},{7,13},{8,14},{9,15},... | collective-permute-start | bytes 442376
  1490.4 102.3 %collective-permute-start.17 = (bf16[24,3072]{1,0:T(8,128)(2,1)}, bf16[24,3072]{1,0:T(8,128)(2,1)}, u32[]{:S(2)}, u32[]{:S(2)}) collective-permute-start(bf16[24,3072]{1,0:T(8,128)(2,1)} %convert.125), channel_id=1, source_target_pairs={{0,7},{1,8},{2,9},{3,10},{4,11},{5,12},{6,13},{7,14},{8,15},{9,16}... | collective-permute-start | bytes 442376
  1493.4 99.3 %collective-permute-start.18 = (bf16[24,3072]{1,0:T(8,128)(2,1)}, bf16[24,3072]{1,0:T(8,128)(2,1)}, u32[]{:S(2)}, u32[]{:S(2)}) collective-permute-start(bf16[24,3072]{1,0:T(8,128)(2,1)} %convert.125), channel_id=1, source_target_pairs={{0,8},{1,9},{2,10},{3,11},{4,12},{5,13},{6,14},{7,15},{8,16},{9,17... | collective-permute-start | bytes 442376
  1498.7 94.1 %collective-permute-start.19 = (bf16[24,3072]{1,0:T(8,128)(2,1)}, bf16[24,3072]{1,0:T(8,128)(2,1)}, u32[]{:S(2)}, u32[]{:S(2)}) collective-permute-start(bf16[24,3072]{1,0:T(8,128)(2,1)} %convert.125), channel_id=1, source_target_pairs={{0,9},{1,10},{2,11},{3,12},{4,13},{5,14},{6,15},{7,16},{8,17},{9,1... | collective-permute-start | bytes 442376
  1501.3 91.4 %collective-permute-start.20 = (bf16[24,3072]{1,0:T(8,128)(2,1)}, bf16[24,3072]{1,0:T(8,128)(2,1)}, u32[]{:S(2)}, u32[]{:S(2)}) collective-permute-start(bf16[24,3072]{1,0:T(8,128)(2,1)} %convert.125), channel_id=1, source_target_pairs={{0,10},{1,11},{2,12},{3,13},{4,14},{5,15},{6,16},{7,17},{8,18},{9,... | collective-permute-start | bytes 442376
  1811.9 198.2 %all-gather.12.cloned.1.call-start = ((), (), s32[]{:S(2)}) async-start(), calls=%async_computation.3 | async-start | bytes 15974400 | tf_op jit(solution)/reshape | solution.py:58
  1814.8 298.7 %all-gather.10.cloned.1.call-start = ((), (), s32[]{:S(2)}) async-start(), calls=%async_computation.2 | async-start | bytes 15974400 | tf_op jit(solution)/reshape | solution.py:58
  (46 other events, 3931.3 us)
Sparse Core Ops, SparseCore 0:
  288.5 561.5 reduce-scatter.24
  854.8 574.1 reduce-scatter.22
  1812.0 94.7 all-gather.13
  1910.1 99.9 all-gather.11
  2013.4 99.9 all-gather.9
where the time goes:
time: 2160 us; the launch traced here: 2140 us
  blocking collectives  1060 us (49%)
  matrix products  374 us (17%)
  waiting for transfers between devices  276 us (13%)
  local copies, waits for them, and re-layouts  185 us (9%)
  starting transfers between devices  163 us (8%)
  other arithmetic  64 us (3%)
    unnamed x2, blocking collectives  889 us
    reshape x3, waiting for transfers between devices, step(): t.reshape(-1, *t.shape[2:])  276 us
    unnamed x75, local copies, waits for them, and re-layouts  180 us
    reduce_sum x1, blocking collectives, of_a_group(): jnp.sum(g * g)  174 us
    unnamed x46, starting transfers between devices  163 us
    dot_general x5, matrix products, layer(): up = jnp.dot(a, w['w_up'], preferred_element_type=jnp.float32)  127 us
    dot_general x5, matrix products, layer(): gate = jnp.dot(a, w['w_gate'], preferred_element_type=jnp.float32)  125 us
    dot_general x5, matrix products, matmul(): jnp.dot(a, w, preferred_element_type=jnp.float32).astype(jnp.bfloat16)  121 us
  transfers between devices with their start and end apart: 49, of which 3 were waited for; matrix products, arithmetic and copies ran while one was open for 56% of the time, Pallas kernels for 0%

commit v1 on v0

v1 whole, which is shorter than its diff:
```python
import functools
import math

import jax
import jax.numpy as jnp
from jax import lax
from jax.experimental import pallas as pl
from jax.experimental.pallas import tpu as pltpu
from jax.sharding import PartitionSpec as P

MESH = pl.DeviceIdType.MESH
F32, BF16 = jnp.float32, jnp.bfloat16
AXES = ("x", "y", "z")
ORDER = ((0, 1, 2), (1, 2, 0), (2, 0, 1))
COLOURS = range(3)
NEAR, ALL = (1, 3), (1, 2, 3)
STEPS = 3
VMEM_LIMIT = 67043328
ROWS, PIECE, WIDE = 80, 256, 1024
LOW, HALF = 16, 640
SHARE = 20
DMA = pltpu.SemaphoreType.DMA


def position():
    return tuple(lax.axis_index(axis) for axis in AXES)


def peer(c, axis, delta):
    return {AXES[axis]: (c[axis] + delta) % 4}


def greet(c, deltas):
    barrier = pltpu.get_barrier_semaphore()
    for axis in range(3):
        for delta in deltas[axis]:
            pl.semaphore_signal(barrier, inc=1, device_id=peer(c, axis, delta), device_id_type=MESH)
    pl.semaphore_wait(barrier, sum(len(d) for d in deltas))


def along(c, axis, d, steps):
    return (c[axis] + 4 - steps + d * (2 * steps - 4)) % 4


def lanes(start, size):
    return pl.ds(start if isinstance(start, int) else pl.multiple_of(start, 128), size)


def loop(n, body):
    lax.fori_loop(0, n, lambda j, carry: (body(j), carry)[1], 0)


def whole_or(index):
    return pl.ds(0, 4) if index is None else pl.ds(index, 1)


def lead_of(sel, relative):
    return tuple(pl.ds(0, 1) if relative is not None and not relative[i] else whole_or(s) for i, s in enumerate(sel))


def columns_of(k, z):
    return lanes(WIDE * k + PIECE * z, PIECE)


class Wide:
    @staticmethod
    def shape(free, halves):
        return (*(4 if f else 1 for f in free[:2]), ROWS, (WIDE if free[2] else PIECE) // halves)

    @staticmethod
    def box(k, sel, half, relative=None):
        wide = (WIDE if sel[2] is None else PIECE) // 2
        start = (WIDE * k if relative is None else 0) + half * wide
        if sel[2] is not None and (relative is None or relative[2]):
            start = start + sel[2] * PIECE
        return (*lead_of(sel[:2], relative), pl.ds(0, ROWS), lanes(start, wide))


class Down:
    @staticmethod
    def shape(free, halves):
        return (*(4 if f else 1 for f in free), LOW, 2 * HALF // halves)

    @staticmethod
    def box(k, sel, half, relative=None):
        return (*lead_of(sel, relative), *(() if relative is not None else (k,)), pl.ds(0, LOW), lanes(half * HALF, HALF))


def free_after(k, phases):
    return tuple(axis not in ORDER[k][:phases] for axis in range(3))


def each(lead, body):
    n = math.prod(lead)

    def at(j, carry):
        index = []
        for size in reversed(lead):
            index.append(j % size if size > 1 else 0)
            j = j // size
        body(tuple(reversed(index)))
        return carry

    if n == 1:
        body((0,) * len(lead))
    else:
        lax.fori_loop(0, n, at, 0)


KINDS = (Wide, Wide, Wide, Down)
TURNS = {kind: tuple((s, n) for s in range(1, STEPS + 1) for n, other in enumerate(KINDS) if other is kind) for kind in (Wide, Down)}


def scatter_scratch():
    shapes = []
    for kind in TURNS:
        for k in COLOURS:
            shapes.append(pltpu.VMEM((2, 2, *kind.shape(free_after(k, 1), 2)), BF16))
    for kind in KINDS:
        for k in COLOURS:
            for p in range(3):
                shapes.append(pltpu.VMEM((2, STEPS, *kind.shape(free_after(k, p + 1), 2)), BF16))
            for p in (1, 2):
                shapes.append(pltpu.VMEM((2, *kind.shape(free_after(k, p + 1), 2)), BF16))
            for p in range(2):
                shapes.append(pltpu.VMEM(kind.shape(free_after(k, p + 1), 1), F32))
    return shapes


def scatter_kernel(*refs):
    refs = iter(refs)
    take = lambda n: [next(refs) for _ in range(n)]
    sources, moments = take(len(KINDS)), take(4)
    outs, (spread,) = take(len(KINDS)), take(1)
    stage, held, first, total = {}, {}, {}, {}
    for kind in TURNS:
        for k in COLOURS:
            stage[kind, k] = next(refs)
    for n in range(len(KINDS)):
        for k in COLOURS:
            for p in range(3):
                held[n, k, p] = next(refs)
            for p in (1, 2):
                first[n, k, p] = next(refs)
            for p in range(2):
                total[n, k, p] = next(refs)
    send_sem, recv_sem, stage_sem, send_moment, recv_moment, local_sem = refs
    c = position()
    greet(c, (NEAR, NEAR, ALL))

    def hop(n, k, d, p, s, source=None):
        to = held[n, k, p].at[d, s]
        return pltpu.make_async_remote_copy(
            src_ref=to if source is None else source,
            dst_ref=to,
            send_sem=send_sem.at[n, 2 * k + d, p, s],
            recv_sem=recv_sem.at[n, 2 * k + d, p, s],
            device_id=peer(c, ORDER[k][p], 1 + 2 * d),
            device_id_type=MESH,
        )

    def selected(k, p, target):
        sel = [None] * 3
        for axis in ORDER[k][:p]:
            sel[axis] = c[axis]
        sel[ORDER[k][p]] = target
        return sel

    def term(kind, k, d, turn):
        s, n = TURNS[kind][turn]
        box = kind.box(k, selected(k, 0, along(c, ORDER[k][0], d, s + 1)), d)
        slot = turn % 2
        return pltpu.make_async_copy(sources[n].at[box], stage[kind, k].at[d, slot], stage_sem.at[int(kind is Down), 2 * k + d, slot])

    def own(n, k, d, p, s):
        kind = KINDS[n]
        if p == 0:
            turn = TURNS[kind].index((s, n))
            term(kind, k, d, turn).wait()
            return stage[kind, k].at[d, turn % 2]
        target = along(c, ORDER[k][p], d, s + 1)
        return total[n, k, p - 1].at[kind.box(k, selected(k, p, target), d, free_after(k, p))]

    def step(n, k, d, p, s):
        kind = KINDS[n]
        shape = kind.shape(free_after(k, p + 1), 2)
        lead, wide = shape[:-2], shape[-1]
        if s == 0 and p == 0:
            hop(n, k, d, p, s, sources[n].at[kind.box(k, selected(k, 0, along(c, ORDER[k][0], d, 1)), d)]).start()
            return
        mine = own(n, k, d, p, s)
        if s == 0:
            out = first[n, k, p].at[d]
            each(lead, lambda i: out.__setitem__(i, mine[i].astype(BF16)))
            hop(n, k, d, p, s, out).start()
            return
        hop(n, k, d, p, s - 1).wait_recv()
        come = held[n, k, p].at[d, s - 1]

        def both(i):
            return come[i].astype(F32) + mine[i].astype(F32)

        if s < STEPS:
            each(lead, lambda i: come.__setitem__(i, both(i).astype(BF16)))
            hop(n, k, d, p, s, come).start()
        elif p < 2:
            out = total[n, k, p]
            each(lead, lambda i: out.__setitem__((*i, slice(None), lanes(d * wide, wide)), both(i)))
        elif kind is Wide:
            outs[n][:, lanes(PIECE * k + wide * d, wide)] = both((0, 0)).astype(BF16)
        else:
            outs[n][k, :, lanes(wide * d, wide)] = both((0, 0, 0)).astype(BF16)
        turn = TURNS[kind].index((s, n)) + 2
        if p == 0 and turn < len(TURNS[kind]):
            term(kind, k, d, turn).start()

    def exchange(j, k, delta):
        return pltpu.make_async_remote_copy(
            src_ref=moments[j].at[:, :, columns_of(k, (c[2] + delta + 1) % 4)],
            dst_ref=spread.at[j, :, c[2], :, pl.ds(PIECE * k, PIECE)],
            send_sem=send_moment.at[j, k, delta],
            recv_sem=recv_moment.at[j, k, delta],
            device_id=peer(c, 2, delta + 1),
            device_id_type=MESH,
        )

    def keep(j, k):
        return pltpu.make_async_copy(
            moments[j].at[:, :, columns_of(k, c[2])], spread.at[j, :, c[2], :, pl.ds(PIECE * k, PIECE)], local_sem.at[j, k]
        )

    pieces = [(j, k) for j in range(4) for k in COLOURS]
    for kind in TURNS:
        for k in COLOURS:
            for turn in range(2):
                loop(2, lambda d: term(kind, k, d, turn).start())
    for slot in range(10):
        phase, s = slot // 3, slot % 3
        for n in range(len(KINDS)):
            for p, s_of in ((phase - 1, STEPS), (phase, 0)) if s == 0 else ((phase, s),):
                if 0 <= p < 3:
                    for k in COLOURS:
                        loop(2, lambda d: step(n, k, d, p, s_of))
        if slot == 4:
            for j, k in pieces:
                loop(3, lambda delta: exchange(j, k, delta).start())
                keep(j, k).start()
    for j, k in pieces:
        loop(3, lambda delta: exchange(j, k, delta).wait())
        keep(j, k).wait()
    for n in range(len(KINDS)):
        for k in COLOURS:
            for p in range(3):
                loop(2 * STEPS, lambda i: hop(n, k, i % 2, p, i // 2).wait_send())


ANYWHERE = pl.BlockSpec(memory_space=pl.ANY)
WHOLE = pl.BlockSpec(memory_space=pltpu.VMEM)


def params(number):
    return pltpu.CompilerParams(collective_id=number, has_side_effects=True, vmem_limit_bytes=VMEM_LIMIT)


def scatter(gradients, moments):
    count = len(KINDS)
    steps = (count, 6, 3, STEPS)
    return pl.pallas_call(
        scatter_kernel,
        out_shape=[jax.ShapeDtypeStruct((ROWS, 3 * PIECE) if kind is Wide else (3, LOW, 2 * HALF), BF16) for kind in KINDS]
        + [jax.ShapeDtypeStruct((4, 2, 4, SHARE, 3 * PIECE), F32)],
        in_specs=[ANYWHERE] * (count + 4),
        out_specs=[WHOLE] * count + [ANYWHERE],
        scratch_shapes=scatter_scratch() + [DMA(steps), DMA(steps), DMA((2, 6, 2)), DMA((4, 3, 3)), DMA((4, 3, 3)), DMA((4, 3))],
        compiler_params=params(1),
        cost_estimate=pl.CostEstimate(flops=10**11, bytes_accessed=10**8, transcendentals=0),
        name="scatter",
    )(*gradients, *moments)


def finish_kernel(count, *refs):
    refs = iter(refs)
    take = lambda n: [next(refs) for _ in range(n)]
    g = [take(3), take(3)]
    spread, m_d, v_d = take(3)
    w, outs = take(3), take(3)
    nmv, nm_d, nv_d = take(3)
    news, (g_wide, w_wide, spread_new, sums, mine) = take(3), take(5)
    send_sem, recv_sem, local_sem, send_sum, recv_sum, send_moment, recv_moment, local_moment = refs
    c = position()
    greet(c, (ALL, ALL, ALL))

    part = jnp.zeros((8, 128), F32)
    for layer in range(2):
        for n in range(2):
            for i in range(6):
                span = slice(128 * i, 128 * i + 128)
                block = g[layer][n][:, span].astype(F32)
                g_wide[layer, n, :, span] = block
                part = part + jnp.sum((block * block).reshape(ROWS // 8, 8, 128), axis=0)
        for i in range(10):
            block = g[layer][2][:, :, 128 * i : 128 * i + 128].astype(F32)
            part = part + jnp.sum((block * block).reshape(6, 8, 128), axis=0)
    for axis in range(3):
        mine[axis] = part
        sums[axis, c[axis]] = part
        copies = [
            pltpu.make_async_remote_copy(
                src_ref=mine.at[axis],
                dst_ref=sums.at[axis, c[axis]],
                send_sem=send_sum.at[axis, delta - 1],
                recv_sem=recv_sum.at[axis, delta - 1],
                device_id=peer(c, axis, delta),
                device_id_type=MESH,
            )
            for delta in ALL
        ]
        for copy in copies:
            copy.start()
        for copy in copies:
            copy.wait()
        part = (sums[axis, 0] + sums[axis, 1]) + (sums[axis, 2] + sums[axis, 3])
    square = jnp.sum(jnp.sum(part, axis=0, keepdims=True), axis=1, keepdims=True)
    factor = jnp.minimum(1.0, 0.5 * lax.rsqrt(square / count + 1e-30))

    def adamw(w, m, v, g):
        g = g * factor
        m = 0.9 * m + 0.1 * g
        v = 0.95 * v + 0.05 * g * g
        return w - 0.02 * (m * lax.rsqrt(v + 1e-8) + 0.1 * w), m, v

    for layer in range(2):
        for k in COLOURS:
            span = slice(PIECE * k, PIECE * k + PIECE)
            for n in range(2):
                w_wide[layer, n, :, span] = w[n][layer, :, span].astype(F32)
                for z in range(4):
                    rows = slice(SHARE * z, SHARE * z + SHARE)
                    new, m, v = adamw(
                        w_wide[layer, n, rows, span], spread[n, layer, z, :, span], spread[n + 2, layer, z, :, span], g_wide[layer, n, rows, span]
                    )
                    w_wide[layer, n, rows, span] = new
                    spread_new[n, layer, z, :, span] = m
                    spread_new[n + 2, layer, z, :, span] = v
                news[n][layer, 0, 0, :, span] = w_wide[layer, n, :, span].astype(BF16)
            new, m, v = adamw(w[2][layer, k].astype(F32), m_d[layer, k], v_d[layer, k], g[layer][2][k].astype(F32))
            news[2][layer, 0, 0, 0, k] = new.astype(BF16)
            nm_d[layer, k] = m
            nv_d[layer, k] = v

    kinds = (Wide, Wide, Down)

    def hop(n, k, d, p, s, local=False):
        axis = ORDER[k][2 - p]
        sel = [None] * 3
        for other in ORDER[k][: 2 - p]:
            sel[other] = c[other]
        sel[axis] = along(c, axis, d, s)
        box = outs[n].at[(slice(None), *kinds[n].box(k, sel, d))]
        source = box
        if p == 0 and s == 0:
            if n < 2:
                source = news[n].at[:, :, :, :, lanes(PIECE * k + PIECE // 2 * d, PIECE // 2)]
            else:
                source = news[n].at[:, :, :, :, k, :, lanes(HALF * d, HALF)]
        if local:
            return pltpu.make_async_copy(source, box, local_sem.at[n, 2 * k + d])
        return pltpu.make_async_remote_copy(
            src_ref=source,
            dst_ref=box,
            send_sem=send_sem.at[n, 2 * k + d, p, s],
            recv_sem=recv_sem.at[n, 2 * k + d, p, s],
            device_id=peer(c, axis, 1 + 2 * d),
            device_id_type=MESH,
        )

    def go(n, k, d, p, s):
        if p == 0 and s == 0:
            hop(n, k, d, p, s, local=True).start()
        hop(n, k, d, p, s).start()

    def arrived(n, k, d, p, s):
        hop(n, k, d, p, s).wait_recv()
        if p == 0 and s == 2:
            hop(n, k, d, 0, 0, local=True).wait()

    def exchange(k, delta):
        return pltpu.make_async_remote_copy(
            src_ref=spread_new.at[:, :, (c[2] + delta + 1) % 4, :, pl.ds(PIECE * k, PIECE)],
            dst_ref=nmv.at[:, :, :, columns_of(k, c[2])],
            send_sem=send_moment.at[k, delta],
            recv_sem=recv_moment.at[k, delta],
            device_id=peer(c, 2, delta + 1),
            device_id_type=MESH,
        )

    def keep(k):
        return pltpu.make_async_copy(
            spread_new.at[:, :, c[2], :, pl.ds(PIECE * k, PIECE)], nmv.at[:, :, :, columns_of(k, c[2])], local_moment.at[k]
        )

    for slot in range(10):
        for n in range(3):
            for k in COLOURS:
                if slot > 0:
                    loop(2, lambda d: arrived(n, k, d, (slot - 1) // 3, (slot - 1) % 3))
            for k in COLOURS:
                if slot < 9:
                    loop(2, lambda d: go(n, k, d, slot // 3, slot % 3))
        if slot == 0:
            for k in COLOURS:
                loop(3, lambda delta: exchange(k, delta).start())
                keep(k).start()
    for k in COLOURS:
        loop(3, lambda delta: exchange(k, delta).wait())
        keep(k).wait()
    for n in range(3):
        for k in COLOURS:
            for p in range(3):
                for s in range(STEPS):
                    loop(2, lambda d: hop(n, k, d, p, s).wait_send())


def finish(count, gradients, spread, m_d, v_d, weights):
    steps = (3, 6, 3, STEPS)
    block = (2, 1, 1, ROWS, 3 * PIECE)
    small = jax.ShapeDtypeStruct(m_d.shape, F32)
    return pl.pallas_call(
        functools.partial(finish_kernel, count),
        out_shape=[
            jax.ShapeDtypeStruct((2, 4, 4, ROWS, 3 * WIDE), BF16),
            jax.ShapeDtypeStruct((2, 4, 4, ROWS, 3 * WIDE), BF16),
            jax.ShapeDtypeStruct((2, 4, 4, 4, 3, LOW, 2 * HALF), BF16),
            jax.ShapeDtypeStruct((4, 2, SHARE, 3 * WIDE), F32),
            small,
            small,
        ],
        in_specs=[WHOLE] * 12,
        out_specs=[ANYWHERE] * 4 + [WHOLE] * 2,
        scratch_shapes=[
            pltpu.VMEM(block, BF16),
            pltpu.VMEM(block, BF16),
            pltpu.VMEM((2, 1, 1, 1, 3, LOW, 2 * HALF), BF16),
            pltpu.VMEM((2, 2, ROWS, 3 * PIECE), F32),
            pltpu.VMEM((2, 2, ROWS, 3 * PIECE), F32),
            pltpu.VMEM(spread.shape, F32),
            pltpu.VMEM((3, 4, 8, 128), F32),
            pltpu.VMEM((3, 8, 128), F32),
            DMA(steps),
            DMA(steps),
            DMA(steps[:2]),
            DMA((3, 3)),
            DMA((3, 3)),
            DMA((3, 3)),
            DMA((3, 3)),
            DMA((3,)),
        ],
        compiler_params=params(2),
        cost_estimate=pl.CostEstimate(flops=10**11, bytes_accessed=10**8, transcendentals=0),
        name="finish",
    )(*gradients, spread, m_d, v_d, *weights)


def dot(a, b, dims):
    return lax.dot_general(a, b, (dims, ((), ())), preferred_element_type=F32)


def normed(h):
    wide = h.astype(F32)
    scale = lax.rsqrt(jnp.mean(wide**2, -1, keepdims=True) + 1e-6)
    return (wide * scale).astype(BF16)


def forward(h, w_gate, w_up):
    a, back = jax.vjp(normed, h)
    gate, up = dot(a, w_gate, ((1,), (0,))), dot(a, w_up, ((1,), (0,)))
    return a, back, gate, up, (jax.nn.silu(gate) * up).astype(BF16)


def hidden_gradient(dy, w_down, gate, up):
    by = dot(dy, w_down, ((1,), (1,))).astype(BF16).astype(F32)
    s = jax.nn.sigmoid(gate)
    return (by * up * (s + gate * s * (1 - s))).astype(BF16), (by * gate * s).astype(BF16)


def weight_gradient(a, d):
    return dot(a, d, ((0,), (0,))).astype(BF16)


def over_x(g):
    return lax.psum_scatter(g, AXES[0], scatter_dimension=0, tiled=True)


def over_yz(g):
    return lax.psum_scatter(g, AXES[1:], scatter_dimension=0, tiled=False)


def body(x, dy, w_gate, w_up, w_down, m_gate, m_up, m_down, v_gate, v_up, v_down):
    h, dy = x[0], dy[0]
    c = position()
    first = forward(h, w_gate[0], w_up[0])
    h = h + dot(first[4], w_down[0], ((1,), (0,))).astype(BF16)
    second = forward(h, w_gate[1], w_up[1])

    gradients = []
    for layer, (a, back, gate, up, act) in ((1, second), (0, first)):
        d_down = weight_gradient(act, dy)
        d_gate, d_up = hidden_gradient(dy, w_down[layer], gate, up)
        gradients.append((weight_gradient(a, d_gate), weight_gradient(a, d_up), d_down))
        if layer:
            da = dot(d_gate, w_gate[layer], ((1,), (1,))).astype(BF16) + dot(d_up, w_up[layer], ((1,), (1,))).astype(BF16)
            dy = dy + back(da)[0]

    (gate_1, up_1, down_1), (gate_0, up_0, down_0) = gradients
    down_1 = over_yz(over_x(down_1).reshape(-1, 3, LOW, 2 * HALF))
    gate_1, up_1, gate_0, up_0, down_0 = lax.optimization_barrier((over_x(gate_1), up_1, gate_0, up_0, down_0))
    gate_1 = jnp.moveaxis(gate_1.reshape(4, ROWS, 3, 4, PIECE), 3, 1)
    gate_1 = over_yz(gate_1.reshape(-1, ROWS, 3 * PIECE))

    by_rows = [g.reshape(4, 4, ROWS, 3 * WIDE) for g in (up_1, gate_0, up_0)]
    up_1, gate_0, up_0, down_0, spread = scatter(
        (*by_rows, down_0.reshape(4, 4, 4, 3, LOW, 2 * HALF)), (m_gate, m_up, v_gate, v_up)
    )

    row, rows = 4 * c[0] + c[1], []
    for w in (w_gate, w_up):
        w = lax.dynamic_slice_in_dim(w, ROWS * row, ROWS, axis=1)
        rows.append(jnp.concatenate([lax.dynamic_slice_in_dim(w, WIDE * k + PIECE * c[2], PIECE, axis=2) for k in COLOURS], axis=2))
    by_colour = (2, 3, LOW, 2 * HALF)
    rows.append(lax.dynamic_slice_in_dim(w_down, 3 * LOW * (4 * row + c[2]), 3 * LOW, axis=1).reshape(by_colour))
    count = float(w_gate.size + w_up.size + w_down.size)
    new_gate, new_up, new_down, moments, m_d, v_d = finish(
        count, (gate_0, up_0, down_0, gate_1, up_1, down_1), spread, m_down.reshape(by_colour), v_down.reshape(by_colour), rows
    )
    return (
        new_gate.reshape(w_gate.shape),
        new_up.reshape(w_up.shape),
        new_down.reshape(w_down.shape),
        moments[0],
        moments[1],
        m_d.reshape(m_down.shape),
        moments[2],
        moments[3],
        v_d.reshape(v_down.shape),
    )


def solution(mesh):
    torus = jax.sharding.Mesh(mesh.devices.reshape(2, 4, 4, 4), ("rep", *AXES))
    moment, everywhere = P(None, AXES), ("rep", *AXES)
    return jax.shard_map(
        body,
        mesh=torus,
        in_specs=(P(everywhere),) * 2 + (P(),) * 3 + (moment,) * 6,
        out_specs=(P("rep"),) * 3 + (P("rep", AXES),) * 6,
        check_vma=False,
    )
```

time: 2160 us -> 895 us (0.41)
  blocking collectives: 1060 us -> 0 us
  Pallas kernels: 0 us -> 388 us
  waiting for transfers between devices: 276 us -> 0.11 us
  starting transfers between devices: 163 us -> 0.16 us
  local copies, waits for them, and re-layouts: 185 us -> 79.7 us
  other arithmetic: 64 us -> 17 us
    unnamed x2 -> x0, blocking collectives: 889 us -> none
    pallas_call x0 -> x2, Pallas kernels: none -> 388 us  [the longest x1 209 us: finish(): pl.pallas_call(functools.partial(finish_kernel, count), out_shape=[jax.Sh...]
    reshape x3 -> x0, waiting for transfers between devices: 276 us -> none  [step(): t.reshape(-1, *t.shape[2:])]
    reduce_sum x1 -> x0, blocking collectives: 174 us -> none  [of_a_group(): jnp.sum(g * g)]
    unnamed x46 -> x2, starting transfers between devices: 163 us -> 0.08 us
    unnamed x75 -> x57, local copies, waits for them, and re-layouts: 180 us -> 62.3 us
    unnamed x9 -> x4, other arithmetic: 50.8 us -> 0.01 us
  transfers between devices with their start and end apart: 49 -> 4, of which waited for: 3 -> 0; matrix products, arithmetic and copies ran while one was open for 56% -> 27% of each run, Pallas kernels for 0% -> 20%
where the time goes in v1:
time: 895 us; the launch traced here: 887 us
  matrix products  388 us (43%)
  Pallas kernels  388 us (43%)
  local copies, waits for them, and re-layouts  79.7 us (9%)
  other arithmetic  17 us (2%)
  between operations  14.2 us (2%)
    dot_general x15, matrix products, dot(): return lax.dot_general(a, b, (dims, ((), ())), preferred_element_type=F32)  388 us
    pallas_call x1, Pallas kernels, finish(): pl.pallas_call(functools.partial(finish_kernel, count), out_shape=[jax.Sh...  209 us
    pallas_call x1, Pallas kernels, scatter(): pl.pallas_call(scatter_kernel, out_shape=[jax.ShapeDtypeStruct((ROWS, 3 *...  179 us
    unnamed x57, local copies, waits for them, and re-layouts  62.3 us
  transfers between devices with their start and end apart: 4, of which 0 were waited for; matrix products, arithmetic and copies ran while one was open for 27% of the time, Pallas kernels for 20%

profile of v1, /device:TPU:0, one launch (start us, length us, event | category | flops | bytes accessed | tf_op | source)
XLA Modules:
  0.0 887.4 jit_solution(7409772949889620297)
XLA Ops:
  7.2 8.0 copy.42
  15.2 3.7 fusion.25
  19.0 22.4 %convolution_convert_fusion.4 = bf16[2048,3072]{1,0:T(8,128)(2,1)} fusion(bf16[2,3072,1280]{2,1,0:T(8,128)(2,1)} %param.15, bf16[1,2048,1280]{2,1,0:T(8,128)(2,1)} %param.12), kind=kOutput, calls=%fused_computation.35 | convolution fusion | flops 16112418816 | bytes 25690112 | tf_op jit(solution)/shard_map/dot_general | solution.py:465
  41.4 21.9 %fusion.46 = f32[2048,3072]{1,0:T(8,128)} fusion(bf16[2,1280,3072]{2,1,0:T(8,128)(2,1)} %param.13, bf16[1,2048,1280]{2,1,0:T(8,128)(2,1)S(1)} %bitcast.108, f32[2048]{0:T(1024)S(1)} %add_rsqrt_fusion), kind=kOutput, calls=%fused_computation.59 | convolution fusion | flops 16113991680 | bytes 38281216 | tf_op jit(solution)/shard_map/dot_general | solution.py:465
  63.2 35.0 %multiply_convert_fusion.1 = (bf16[2048,3072]{1,0:T(8,128)(2,1)}, f32[2048,3072]{1,0:T(8,128)}) fusion(f32[2048,3072]{1,0:T(8,128)} %fusion.46, bf16[2,1280,3072]{2,1,0:T(8,128)(2,1)} %param.14, bf16[1,2048,1280]{2,1,0:T(8,128)(2,1)} %param.11, f32[2048]{0:T(1024)S(1)} %add_rsqrt_fusion), kind=kOutput, calls=%fused_computation.14 | convolution fusion | flops 16151740416 | bytes 76029952 | tf_op jit(solution)/shard_map/dot_general | solution.py:465
  98.2 22.5 %fusion.29 = (f32[2048]{0:T(1024)S(1)}, bf16[2048,1280]{0,1:T(8,128)(2,1)S(1)}) fusion(bf16[2048,3072]{1,0:T(8,128)(2,1)} %get-tuple-element.80, bf16[2,3072,1280]{2,1,0:T(8,128)(2,1)} %param.15, bf16[1,2048,1280]{1,2,0:T(8,128)(2,1)} %copy.42), kind=kOutput, calls=%fused_computation.41 | convolution fusion | flops 16119232512 | bytes 30941184 | tf_op jit(solution)/shard_map/dot_general | solution.py:465
  121.3 1.8 copy-done
  123.1 22.5 %fusion.38 = f32[2048,3072]{1,0:T(8,128)} fusion(bf16[2,1280,3072]{2,1,0:T(8,128)(2,1)} %param.14, bf16[2048,1280]{0,1:T(8,128)(2,1)S(1)} %get-tuple-element.83, f32[2048]{0:T(1024)S(1)} %fusion.84), kind=kOutput, calls=%fused_computation.51 | convolution fusion | flops 16113991680 | bytes 38281216 | tf_op jit(solution)/shard_map/dot_general | solution.py:465
  145.6 42.6 %fusion.3 = (bf16[2048,3072]{1,0:T(8,128)(2,1)}, bf16[2048,3072]{1,0:T(8,128)(2,1)}, f32[2048,3072]{1,0:T(8,128)}) fusion(bf16[2048,3072]{1,0:T(8,128)(2,1)} %convolution_convert_fusion.4, f32[2048,3072]{1,0:T(8,128)} %fusion.38, bf16[2,1280,3072]{2,1,0:T(8,128)(2,1)} %param.13, bf16[2048,1280]{0,1:T(8,128)(2,1)} %copy-done, f32[2048]{0:T(1024)S(1)} %fusion.84), kind=kOutput, calls=%fused_computation.7 | convolution fusion | flops 16202072064 | bytes 101195776 | tf_op jit(solution)/shard_map/dot_general | solution.py:465
  188.2 22.3 %convolution_convert_fusion.3 = bf16[1280,3072]{1,0:T(8,128)(2,1)} fusion(bf16[2048,3072]{1,0:T(8,128)(2,1)} %get-tuple-element.69, bf16[2048,1280]{0,1:T(8,128)(2,1)} %copy-done, f32[2048]{0:T(1024)S(1)} %fusion.84), kind=kOutput, calls=%fused_computation.34 | convolution fusion | flops 16117923840 | bytes 25698304 | tf_op jit(solution)/shard_map/dot_general | solution.py:465
  210.6 28.6 %fusion.21 = bf16[3072,1280]{1,0:T(8,128)(2,1)} fusion(f32[2048,3072]{1,0:T(8,128)} %fusion.38, f32[2048,3072]{1,0:T(8,128)} %get-tuple-element.84, bf16[1,2048,1280]{2,1,0:T(8,128)(2,1)} %param.12), kind=kOutput, calls=%fused_computation.31 | convolution fusion | flops 16147808256 | bytes 63438848 | tf_op jit(solution)/shard_map/dot_general | solution.py:465
  239.2 22.4 %convolution_convert_fusion.2 = bf16[1280,3072]{1,0:T(8,128)(2,1)} fusion(bf16[2048,3072]{1,0:T(8,128)(2,1)} %get-tuple-element.68, bf16[2048,1280]{0,1:T(8,128)(2,1)} %copy-done, f32[2048]{0:T(1024)S(1)} %fusion.84), kind=kOutput, calls=%fused_computation.33 | convolution fusion | flops 16117923840 | bytes 25698304 | tf_op jit(solution)/shard_map/dot_general | solution.py:465
  261.7 22.5 %fusion.54 = bf16[2048,1280]{0,1:T(8,128)(2,1)} fusion(bf16[2048,3072]{1,0:T(8,128)(2,1)} %get-tuple-element.68, bf16[2,1280,3072]{2,1,0:T(8,128)(2,1)} %param.14), kind=kOutput, calls=%fused_computation.65 | convolution fusion | flops 16108748800 | bytes 25690112 | tf_op jit(solution)/shard_map/dot_general | solution.py:465
  284.2 7.9 copy.43
  292.1 24.9 %fusion.31 = (f32[2048]{0:T(1024)S(1)}, bf16[2048,1280]{0,1:T(8,128)(2,1)}) fusion(bf16[2048,1280]{0,1:T(8,128)(2,1)} %copy-done, bf16[2048,1280]{0,1:T(8,128)(2,1)} %fusion.54, bf16[2048,3072]{1,0:T(8,128)(2,1)} %get-tuple-element.69, bf16[2,1280,3072]{2,1,0:T(8,128)(2,1)} %param.13), kind=kOutput, calls=%fused_computation.43 | convolution fusion | flops 16121853952 | bytes 36184064 | tf_op jit(solution)/shard_map/dot_general | solution.py:465
  317.0 12.5 %fusion.73 = bf16[2048,1280]{0,1:T(8,128)(2,1)} fusion(bf16[2048,1280]{0,1:T(8,128)(2,1)} %copy-done, bf16[2048,1280]{0,1:T(8,128)(2,1)} %get-tuple-element.86, bf16[1,2048,1280]{1,2,0:T(8,128)(2,1)} %copy.43, f32[2048]{0:T(1024)S(1)} %multiply_multiply_fusion, f32[2048]{0:T(1024)S(1)} %fusion.84), kind=kLoop, calls=%fused_computation.76 | loop fusion | flops 18350080 | bytes 20987904 | tf_op jit(solution)/shard_map/add | solution.py:512
  329.5 23.6 %convolution_convert_fusion = bf16[3072,1280]{1,0:T(8,128)(2,1)} fusion(bf16[2048,3072]{1,0:T(8,128)(2,1)} %get-tuple-element.80, bf16[2048,1280]{0,1:T(8,128)(2,1)} %fusion.73), kind=kOutput, calls=%fused_computation.30 | convolution fusion | flops 16110059520 | bytes 25690112 | tf_op jit(solution)/shard_map/dot_general | solution.py:465
  353.1 22.2 %convolution_convert_fusion.1 = bf16[2048,3072]{1,0:T(8,128)(2,1)} fusion(bf16[2048,1280]{0,1:T(8,128)(2,1)S(1)} %copy-done.1, bf16[2,3072,1280]{2,1,0:T(8,128)(2,1)} %param.15), kind=kOutput, calls=%fused_computation.32 | convolution fusion | flops 16112418816 | bytes 25690112 | tf_op jit(solution)/shard_map/dot_general | solution.py:465
  375.3 23.8 %fusion.18 = bf16[1280,3072]{1,0:T(8,128)(2,1)} fusion(f32[2048,3072]{1,0:T(8,128)} %fusion.46, bf16[2048,3072]{1,0:T(8,128)(2,1)} %convolution_convert_fusion.1, bf16[1,2048,1280]{1,2,0:T(8,128)(2,1)S(1)} %bitcast.98, f32[2048]{0:T(1024)S(1)} %copy-done.8), kind=kOutput, calls=%fused_computation.29 | convolution fusion | flops 16161964032 | bytes 50864128 | tf_op jit(solution)/shard_map/dot_general | solution.py:465
  399.1 30.9 %fusion.22 = bf16[1280,3072]{1,0:T(8,128)(2,1)} fusion(f32[2048,3072]{1,0:T(8,128)} %get-tuple-element.81, bf16[2048,3072]{1,0:T(8,128)(2,1)} %convolution_convert_fusion.1, f32[2048,3072]{1,0:T(8,128)} %fusion.46, bf16[1,2048,1280]{1,2,0:T(8,128)(2,1)} %copy.42, f32[2048]{0:T(1024)S(1)} %copy-done.8), kind=kOutput, calls=%fused_computation.36 | convolution fusion | flops 16187129856 | bytes 76029952 | tf_op jit(solution)/shard_map/dot_general | solution.py:465
  430.1 5.1 reshape.107
  435.1 2.7 copy.54
  437.8 3.6 reshape.108
  442.5 2.0 copy.45.refs_5_
  444.5 2.0 copy.46.refs_6_
  446.5 2.0 copy.47.refs_7_
  453.5 179.2 %scatter.1 = (bf16[80,768]{1,0:T(8,128)(2,1)}, bf16[80,768]{1,0:T(8,128)(2,1)}, bf16[80,768]{1,0:T(8,128)(2,1)}, bf16[3,16,1280]{2,1,0:T(8,128)(2,1)}, f32[4,2,4,20,768]{4,3,2,1,0:T(8,128)}) custom-call(bf16[4,4,80,3072]{3,2,1,0:T(8,128)(2,1)} %bitcast.117, bf16[4,4,80,3072]{3,2,1,0:T(8,128)(2,1)} %bitcast.120, bf16[4,4,80,3072]{3,2,1,0:T(8,128)(2,1)} %bitcast.119, ...), custom_call_target="tpu_custom_call" | custom-call | flops 99999997952 | bytes 100000000 | tf_op jit(solution)/shard_map/scatter/pallas_call | solution.py:268
  632.7 208.9 %finish.1 = (bf16[2,4,4,80,3072]{4,3,2,1,0:T(8,128)(2,1)}, bf16[2,4,4,80,3072]{4,3,2,1,0:T(8,128)(2,1)}, bf16[2,4,4,4,3,16,1280]{6,5,4,3,2,1,0:T(8,128)(2,1)}, f...) custom-call(bf16[80,768]{1,0:T(8,128)(2,1)} %get-tuple-element.29.refs_0_, ...), custom_call_target="tpu_custom_call" | custom-call | flops 99999997952 | bytes 100000000 | tf_op jit(solution)/shard_map/finish/pallas_call | solution.py:428
  841.7 1.9 slice_bitcast_fusion
  848.2 15.9 %copy.60 = bf16[2,1280,3072]{2,1,0:T(8,128)(2,1)} copy(bf16[2,1280,3072]{2,1,0:T(8,128)(2,1)} %bitcast.105) | data formatting | bytes 31457280
  864.2 7.9 copy.61
  873.3 5.8 copy.62
  (71 shorter events, 14.2 us)
Async XLA Ops:
  7.2 422.9 %reduce-scatter.9.cloned.1.call-start = ((), (), s32[]{:S(2)}) async-start(), calls=%async_computation.4 | async-start | bytes 9830400 | tf_op jit(solution)/shard_map/reduce_scatter | solution.py:491
  15.2 26.2 %slice-start.10 = ((s8[5242880]{0:T(1024)(128)(4,1)}), s8[4194304]{0:T(1024)(128)(4,1)S(1)}, s32[]{:S(2)}) async-start(s8[5242880]{0:T(1024)(128)(4,1)} %bitcast.107), calls=%async_computation.18 | async-start | bytes 8388608
  19.0 44.3 %copy-start.7 = (f32[2048]{0:T(1024)}, f32[2048]{0:T(1024)S(1)}, u32[]{:S(2)}) copy-start(f32[2048]{0:T(1024)S(1)} %add_rsqrt_fusion) | copy-start | bytes 24580
  19.0 22.4 %slice-start.11 = ((s8[5242880]{0:T(1024)(128)(4,1)}), s8[1048576]{0:T(1024)(128)(4,1)S(1)}, s32[]{:S(2)}) async-start(s8[5242880]{0:T(1024)(128)(4,1)} %bitcast.107), calls=%async_computation.19 | async-start | bytes 2097152
  120.7 0.6 copy-start.5
  120.7 2.4 copy-start
  210.5 242.9 %reduce-scatter.11.cloned.1.call-start = ((), (), s32[]{:S(2)}) async-start(), calls=%async_computation.5 | async-start | bytes 9830400 | tf_op jit(solution)/shard_map/reduce_scatter | solution.py:491
  239.2 393.5 %reduce-scatter.13.cloned.1.call-start = ((), (), s32[]{:S(2)}) async-start(), calls=%async_computation.6 | async-start | bytes 2088960
  292.1 24.9 %copy-start.6 = (f32[2048]{0:T(1024)S(1)}, f32[2048]{0:T(1024)}, u32[]{:S(2)}) copy-start(f32[2048]{0:T(1024)} %copy-done.5) | copy-start | bytes 24580
  317.0 58.3 %slice-start = ((s8[5242880]{0:T(1024)(128)(4,1)}), s8[1048576]{0:T(1024)(128)(4,1)S(1)}, s32[]{:S(2)}) async-start(s8[5242880]{0:T(1024)(128)(4,1)} %bitcast.97), calls=%async_computation.8 | async-start | bytes 2097152
  329.5 23.6 %copy-start.1 = (bf16[2048,1280]{0,1:T(8,128)(2,1)S(1)}, bf16[2048,1280]{0,1:T(8,128)(2,1)}, u32[]{:S(2)}) copy-start(bf16[2048,1280]{0,1:T(8,128)(2,1)} %fusion.73) | copy-start | bytes 15728644
  329.5 45.8 %slice-start.1 = ((s8[5242880]{0:T(1024)(128)(4,1)}), s8[4194304]{0:T(1024)(128)(4,1)S(1)}, s32[]{:S(2)}) async-start(s8[5242880]{0:T(1024)(128)(4,1)} %bitcast.97), calls=%async_computation.9 | async-start | bytes 8388608
  353.1 22.2 %copy-start.8 = (f32[2048]{0:T(1024)S(1)}, f32[2048]{0:T(1024)}, u32[]{:S(2)}) copy-start(f32[2048]{0:T(1024)} %copy-done.7) | copy-start | bytes 24580
  430.0 11.5 %copy-start.2 = (f32[2,20,3072]{2,0,1:T(2,128)S(1)}, f32[2,20,3072]{2,0,1:T(2,128)}, u32[]{:S(2)}) copy-start(f32[2,20,3072]{2,0,1:T(2,128)} %param.16) | copy-start | bytes 1474564
  441.4 191.3 %reduce-scatter.15.cloned.1.call-start = ((), (), s32[]{:S(2)}) async-start(), calls=%async_computation.7 | async-start | bytes 2088960
  841.7 22.5 %slice-start.6 = ((s8[15728640]{0:T(1024)(128)(4,1)}), s8[4194304]{0:T(1024)(128)(4,1)S(1)}, s32[]{:S(2)}) async-start(s8[15728640]{0:T(1024)(128)(4,1)} %bitcast.102), calls=%async_computation.14 | async-start | bytes 8388608
  848.2 15.9 %slice-start.7 = ((s8[15728640]{0:T(1024)(128)(4,1)}), s8[4194304]{0:T(1024)(128)(4,1)S(1)}, s32[]{:S(2)}) async-start(s8[15728640]{0:T(1024)(128)(4,1)} %bitcast.102), calls=%async_computation.15 | async-start | bytes 8388608
  848.2 15.9 %slice-start.8 = ((s8[15728640]{0:T(1024)(128)(4,1)}), s8[4194304]{0:T(1024)(128)(4,1)S(1)}, s32[]{:S(2)}) async-start(s8[15728640]{0:T(1024)(128)(4,1)} %bitcast.102), calls=%async_computation.16 | async-start | bytes 8388608
  848.2 15.9 %slice-start.9 = ((s8[15728640]{0:T(1024)(128)(4,1)}), s8[3145728]{0:T(1024)(128)(4,1)S(1)}, s32[]{:S(2)}) async-start(s8[15728640]{0:T(1024)(128)(4,1)} %bitcast.102), calls=%async_computation.17 | async-start | bytes 6291456
  848.2 23.9 %slice-start.2 = ((s8[15728640]{0:T(1024)(128)(4,1)}), s8[4194304]{0:T(1024)(128)(4,1)S(1)}, s32[]{:S(2)}) async-start(s8[15728640]{0:T(1024)(128)(4,1)} %bitcast.99), calls=%async_computation.10 | async-start | bytes 8388608
  848.2 23.9 %slice-start.3 = ((s8[15728640]{0:T(1024)(128)(4,1)}), s8[4194304]{0:T(1024)(128)(4,1)S(1)}, s32[]{:S(2)}) async-start(s8[15728640]{0:T(1024)(128)(4,1)} %bitcast.99), calls=%async_computation.11 | async-start | bytes 8388608
  864.2 8.0 slice-start.4
  864.2 9.1 %slice-start.5 = ((s8[15728640]{0:T(1024)(128)(4,1)}), s8[3145728]{0:T(1024)(128)(4,1)S(1)}, s32[]{:S(2)}) async-start(s8[15728640]{0:T(1024)(128)(4,1)} %bitcast.99), calls=%async_computation.13 | async-start | bytes 6291456
  873.3 5.8 copy-start.4
  873.3 6.6 copy-start.3
Sparse Core Ops, SparseCore 0:
  210.6 79.3 reduce-scatter.8
  292.4 76.5 reduce-scatter.10
  441.6 80.3 reduce-scatter.12
  525.0 79.6 reduce-scatter.14

commit v2 on v1

--- a/solution.py
+++ b/solution.py
@@ -509,11 +509,11 @@
         gradients.append((weight_gradient(a, d_gate), weight_gradient(a, d_up), d_down))
         if layer:
             da = dot(d_gate, w_gate[layer], ((1,), (1,))).astype(BF16) + dot(d_up, w_up[layer], ((1,), (1,))).astype(BF16)
-            dy = dy + back(da)[0]
-
-    (gate_1, up_1, down_1), (gate_0, up_0, down_0) = gradients
-    down_1 = over_yz(over_x(down_1).reshape(-1, 3, LOW, 2 * HALF))
-    gate_1, up_1, gate_0, up_0, down_0 = lax.optimization_barrier((over_x(gate_1), up_1, gate_0, up_0, down_0))
+            down_1, dy = lax.optimization_barrier((over_x(d_down), dy + back(da)[0]))
+            down_1 = over_yz(down_1.reshape(-1, 3, LOW, 2 * HALF))
+
+    (gate_1, up_1, _), (gate_0, up_0, down_0) = gradients
+    gate_1, gate_0, up_0 = lax.optimization_barrier((over_x(gate_1), gate_0, up_0))
     gate_1 = jnp.moveaxis(gate_1.reshape(4, ROWS, 3, 4, PIECE), 3, 1)
     gate_1 = over_yz(gate_1.reshape(-1, ROWS, 3 * PIECE))
 

time: 895 us -> 894 us (level)
    unnamed x57 -> x63, local copies, waits for them, and re-layouts: 62.3 us -> 60.1 us
  transfers between devices with their start and end apart: 4 -> 4, of which waited for: 0 -> 0; matrix products, arithmetic and copies ran while one was open for 27% -> 26% of each run, Pallas kernels for 20% -> 20%
where the time goes in v2:
time: 894 us; the launch traced here: 885 us
  matrix products  391 us (44%)
  Pallas kernels  384 us (43%)
  local copies, waits for them, and re-layouts  78.5 us (9%)
  other arithmetic  17.6 us (2%)
  between operations  14.5 us (2%)
    dot_general x15, matrix products, dot(): return lax.dot_general(a, b, (dims, ((), ())), preferred_element_type=F32)  391 us
    pallas_call x1, Pallas kernels, finish(): pl.pallas_call(functools.partial(finish_kernel, count), out_shape=[jax.Sh...  209 us
    pallas_call x1, Pallas kernels, scatter(): pl.pallas_call(scatter_kernel, out_shape=[jax.ShapeDtypeStruct((ROWS, 3 *...  175 us
    unnamed x63, local copies, waits for them, and re-layouts  60.1 us
  transfers between devices with their start and end apart: 4, of which 0 were waited for; matrix products, arithmetic and copies ran while one was open for 26% of the time, Pallas kernels for 20%

profile of v2, /device:TPU:0, one launch (start us, length us, event | category | flops | bytes accessed | tf_op | source)
XLA Modules:
  0.0 885.3 jit_solution(9221006126716315516)
XLA Ops:
  7.2 8.0 copy.42
  15.2 3.6 fusion.25
  18.8 23.0 %fusion.46 = f32[2048,3072]{1,0:T(8,128)} fusion(bf16[2,1280,3072]{2,1,0:T(8,128)(2,1)} %param.13, bf16[1,2048,1280]{2,1,0:T(8,128)(2,1)} %param.11, f32[2048]{0:T(1024)S(1)} %add_rsqrt_fusion), kind=kOutput, calls=%fused_computation.59 | convolution fusion | flops 16113991680 | bytes 38281216 | tf_op jit(solution)/shard_map/dot_general | solution.py:465
  41.8 34.7 %multiply_convert_fusion.1 = (bf16[2048,3072]{1,0:T(8,128)(2,1)}, f32[2048,3072]{1,0:T(8,128)}) fusion(f32[2048,3072]{1,0:T(8,128)} %fusion.46, bf16[2,1280,3072]{2,1,0:T(8,128)(2,1)} %param.14, bf16[1,2048,1280]{2,1,0:T(8,128)(2,1)} %param.11, f32[2048]{0:T(1024)S(1)} %add_rsqrt_fusion), kind=kOutput, calls=%fused_computation.14 | convolution fusion | flops 16151740416 | bytes 76029952 | tf_op jit(solution)/shard_map/dot_general | solution.py:465
  76.5 22.7 %fusion.29 = (f32[2048]{0:T(1024)S(1)}, bf16[2048,1280]{0,1:T(8,128)(2,1)S(1)}) fusion(bf16[2048,3072]{1,0:T(8,128)(2,1)} %get-tuple-element.80, bf16[2,3072,1280]{2,1,0:T(8,128)(2,1)} %param.15, bf16[1,2048,1280]{1,2,0:T(8,128)(2,1)} %copy.42), kind=kOutput, calls=%fused_computation.41 | convolution fusion | flops 16119232512 | bytes 30941184 | tf_op jit(solution)/shard_map/dot_general | solution.py:465
  99.3 24.2 %convolution_convert_fusion.4 = bf16[2048,3072]{1,0:T(8,128)(2,1)} fusion(bf16[2,3072,1280]{2,1,0:T(8,128)(2,1)} %param.15, bf16[1,2048,1280]{2,1,0:T(8,128)(2,1)} %param.12), kind=kOutput, calls=%fused_computation.35 | convolution fusion | flops 16112418816 | bytes 25690112 | tf_op jit(solution)/shard_map/dot_general | solution.py:465
  123.4 22.1 %fusion.38 = f32[2048,3072]{1,0:T(8,128)} fusion(bf16[2,1280,3072]{2,1,0:T(8,128)(2,1)} %param.13, bf16[2048,1280]{0,1:T(8,128)(2,1)S(1)} %get-tuple-element.83, f32[2048]{0:T(1024)S(1)} %fusion.84), kind=kOutput, calls=%fused_computation.51 | convolution fusion | flops 16113991680 | bytes 38281216 | tf_op jit(solution)/shard_map/dot_general | solution.py:465
  145.5 42.8 %fusion.3 = (bf16[2048,3072]{1,0:T(8,128)(2,1)}, bf16[2048,3072]{1,0:T(8,128)(2,1)}, f32[2048,3072]{1,0:T(8,128)}) fusion(bf16[2048,3072]{1,0:T(8,128)(2,1)} %convolution_convert_fusion.4, f32[2048,3072]{1,0:T(8,128)} %fusion.38, bf16[2,1280,3072]{2,1,0:T(8,128)(2,1)} %param.14, bf16[2048,1280]{0,1:T(8,128)(2,1)} %copy-done, f32[2048]{0:T(1024)S(1)} %fusion.84), kind=kOutput, calls=%fused_computation.7 | convolution fusion | flops 16202072064 | bytes 101195776 | tf_op jit(solution)/shard_map/dot_general | solution.py:465
  188.3 28.9 %fusion.21 = bf16[3072,1280]{1,0:T(8,128)(2,1)} fusion(f32[2048,3072]{1,0:T(8,128)} %get-tuple-element.84, f32[2048,3072]{1,0:T(8,128)} %fusion.38, bf16[1,2048,1280]{2,1,0:T(8,128)(2,1)} %param.12), kind=kOutput, calls=%fused_computation.31 | convolution fusion | flops 16147808256 | bytes 63438848 | tf_op jit(solution)/shard_map/dot_general | solution.py:465
  217.2 22.2 %convolution_convert_fusion.2 = bf16[1280,3072]{1,0:T(8,128)(2,1)} fusion(bf16[2048,3072]{1,0:T(8,128)(2,1)} %get-tuple-element.68, bf16[2048,1280]{0,1:T(8,128)(2,1)} %copy-done, f32[2048]{0:T(1024)S(1)} %fusion.84), kind=kOutput, calls=%fused_computation.33 | convolution fusion | flops 16117923840 | bytes 25698304 | tf_op jit(solution)/shard_map/dot_general | solution.py:465
  239.5 22.6 %fusion.54 = bf16[2048,1280]{0,1:T(8,128)(2,1)} fusion(bf16[2048,3072]{1,0:T(8,128)(2,1)} %get-tuple-element.68, bf16[2,1280,3072]{2,1,0:T(8,128)(2,1)} %param.13), kind=kOutput, calls=%fused_computation.65 | convolution fusion | flops 16108748800 | bytes 25690112 | tf_op jit(solution)/shard_map/dot_general | solution.py:465
  262.1 8.0 copy.43
  272.0 1.9 constant_dynamic-slice_fusion.6
  273.9 22.4 %convolution_convert_fusion.3 = bf16[1280,3072]{1,0:T(8,128)(2,1)} fusion(bf16[2048,3072]{1,0:T(8,128)(2,1)} %get-tuple-element.69, bf16[2048,1280]{0,1:T(8,128)(2,1)} %copy-done, f32[2048]{0:T(1024)S(1)} %fusion.84), kind=kOutput, calls=%fused_computation.34 | convolution fusion | flops 16117923840 | bytes 25698304 | tf_op jit(solution)/shard_map/dot_general | solution.py:465
  296.3 23.8 %fusion.31 = (f32[2048]{0:T(1024)S(1)}, bf16[2048,1280]{0,1:T(8,128)(2,1)}) fusion(bf16[2048,1280]{0,1:T(8,128)(2,1)S(1)} %bitcast.106, bf16[2048,1280]{0,1:T(8,128)(2,1)S(1)} %copy-done.13, bf16[2048,3072]{1,0:T(8,128)(2,1)} %get-tuple-element.69, bf16[2,1280,3072]{2,1,0:T(8,128)(2,1)} %param.14), kind=kOutput, calls=%fused_computation.43 | convolution fusion | flops 16121853952 | bytes 36184064 | tf_op jit(solution)/shard_map/dot_general | solution.py:465
  320.2 12.3 %fusion.73 = bf16[2048,1280]{0,1:T(8,128)(2,1)} fusion(bf16[2048,1280]{0,1:T(8,128)(2,1)} %copy-done, bf16[2048,1280]{0,1:T(8,128)(2,1)} %get-tuple-element.86, bf16[1,2048,1280]{1,2,0:T(8,128)(2,1)} %copy.43, f32[2048]{0:T(1024)S(1)} %multiply_multiply_fusion, f32[2048]{0:T(1024)S(1)} %fusion.84), kind=kLoop, calls=%fused_computation.76 | loop fusion | flops 18350080 | bytes 20987904 | tf_op jit(solution)/shard_map/add | solution.py:512
  332.5 22.8 %convolution_convert_fusion.1 = bf16[2048,3072]{1,0:T(8,128)(2,1)} fusion(bf16[2048,1280]{0,1:T(8,128)(2,1)} %fusion.73, bf16[2,3072,1280]{2,1,0:T(8,128)(2,1)} %param.15), kind=kOutput, calls=%fused_computation.32 | convolution fusion | flops 16112418816 | bytes 25690112 | tf_op jit(solution)/shard_map/dot_general | solution.py:465
  355.3 24.9 %fusion.18 = bf16[1280,3072]{1,0:T(8,128)(2,1)} fusion(f32[2048,3072]{1,0:T(8,128)} %fusion.46, bf16[2048,3072]{1,0:T(8,128)(2,1)} %convolution_convert_fusion.1, bf16[1,2048,1280]{1,2,0:T(8,128)(2,1)} %copy.42, f32[2048]{0:T(1024)S(1)} %copy-done.12), kind=kOutput, calls=%fused_computation.29 | convolution fusion | flops 16161964032 | bytes 50864128 | tf_op jit(solution)/shard_map/dot_general | solution.py:465
  380.2 31.1 %fusion.22 = bf16[1280,3072]{1,0:T(8,128)(2,1)} fusion(f32[2048,3072]{1,0:T(8,128)} %get-tuple-element.81, bf16[2048,3072]{1,0:T(8,128)(2,1)} %convolution_convert_fusion.1, f32[2048,3072]{1,0:T(8,128)} %fusion.46, bf16[1,2048,1280]{1,2,0:T(8,128)(2,1)} %copy.42, f32[2048]{0:T(1024)S(1)} %copy-done.12), kind=kOutput, calls=%fused_computation.36 | convolution fusion | flops 16187129856 | bytes 76029952 | tf_op jit(solution)/shard_map/dot_general | solution.py:465
  411.4 4.8 reshape.107
  416.1 2.7 copy.54
  418.8 3.6 reshape.108
  425.2 2.0 copy.45.refs_5_
  427.2 2.0 copy.46.refs_6_
  429.2 2.0 copy.47.refs_7_
  432.9 22.5 %convolution_convert_fusion = bf16[3072,1280]{1,0:T(8,128)(2,1)} fusion(bf16[2048,3072]{1,0:T(8,128)(2,1)} %get-tuple-element.80, bf16[2048,1280]{0,1:T(8,128)(2,1)} %fusion.73), kind=kOutput, calls=%fused_computation.30 | convolution fusion | flops 16110059520 | bytes 25690112 | tf_op jit(solution)/shard_map/dot_general | solution.py:465
  455.5 174.8 %scatter.1 = (bf16[80,768]{1,0:T(8,128)(2,1)}, bf16[80,768]{1,0:T(8,128)(2,1)}, bf16[80,768]{1,0:T(8,128)(2,1)}, bf16[3,16,1280]{2,1,0:T(8,128)(2,1)}, f32[4,2,4,20,768]{4,3,2,1,0:T(8,128)}) custom-call(bf16[4,4,80,3072]{3,2,1,0:T(8,128)(2,1)} %bitcast.115, bf16[4,4,80,3072]{3,2,1,0:T(8,128)(2,1)} %bitcast.117, bf16[4,4,80,3072]{3,2,1,0:T(8,128)(2,1)} %bitcast.116, ...), custom_call_target="tpu_custom_call" | custom-call | flops 99999997952 | bytes 100000000 | tf_op jit(solution)/shard_map/scatter/pallas_call | solution.py:268
  630.3 208.9 %finish.1 = (bf16[2,4,4,80,3072]{4,3,2,1,0:T(8,128)(2,1)}, bf16[2,4,4,80,3072]{4,3,2,1,0:T(8,128)(2,1)}, bf16[2,4,4,4,3,16,1280]{6,5,4,3,2,1,0:T(8,128)(2,1)}, f...) custom-call(bf16[80,768]{1,0:T(8,128)(2,1)} %get-tuple-element.28.refs_0_, ...), custom_call_target="tpu_custom_call" | custom-call | flops 99999997952 | bytes 100000000 | tf_op jit(solution)/shard_map/finish/pallas_call | solution.py:428
  839.3 1.9 slice_bitcast_fusion
  845.9 15.9 %copy.60 = bf16[2,1280,3072]{2,1,0:T(8,128)(2,1)} copy(bf16[2,1280,3072]{2,1,0:T(8,128)(2,1)} %bitcast.103) | data formatting | bytes 31457280
  861.8 7.9 copy.61
  870.9 5.8 copy.62
  (76 shorter events, 14.0 us)
Async XLA Ops:
  7.2 325.3 %reduce-scatter.11.cloned.1.call-start = ((), (), s32[]{:S(2)}) async-start(), calls=%async_computation.5 | async-start | bytes 9830400 | tf_op jit(solution)/shard_map/reduce_scatter | solution.py:491
  18.8 23.1 %copy-start.11 = (f32[2048]{0:T(1024)}, f32[2048]{0:T(1024)S(1)}, u32[]{:S(2)}) copy-start(f32[2048]{0:T(1024)S(1)} %add_rsqrt_fusion) | copy-start | bytes 24580
  99.2 24.2 %copy-start.9 = (f32[2048]{0:T(1024)}, f32[2048]{0:T(1024)S(1)}, u32[]{:S(2)}) copy-start(f32[2048]{0:T(1024)S(1)} %get-tuple-element.82) | copy-start | bytes 24580
  99.2 24.2 %copy-start = (bf16[2048,1280]{0,1:T(8,128)(2,1)}, bf16[2048,1280]{0,1:T(8,128)(2,1)S(1)}, u32[]{:S(2)}) copy-start(bf16[2048,1280]{0,1:T(8,128)(2,1)S(1)} %get-tuple-element.83) | copy-start | bytes 15728644
  217.1 194.2 %reduce-scatter.9.cloned.1.call-start = ((), (), s32[]{:S(2)}) async-start(), calls=%async_computation.4 | async-start | bytes 9830400 | tf_op jit(solution)/shard_map/reduce_scatter | solution.py:491
  239.4 390.9 %reduce-scatter.13.cloned.1.call-start = ((), (), s32[]{:S(2)}) async-start(), calls=%async_computation.6 | async-start | bytes 2088960
  262.1 34.2 %slice-start.8 = ((s8[5242880]{0:T(1024)(128)(4,1)}), s8[1048576]{0:T(1024)(128)(4,1)S(1)}, s32[]{:S(2)}) async-start(s8[5242880]{0:T(1024)(128)(4,1)} %bitcast.105), calls=%async_computation.16 | async-start | bytes 2097152
  273.9 22.4 %slice-start.9 = ((s8[5242880]{0:T(1024)(128)(4,1)}), s8[4194304]{0:T(1024)(128)(4,1)S(1)}, s32[]{:S(2)}) async-start(s8[5242880]{0:T(1024)(128)(4,1)} %bitcast.105), calls=%async_computation.17 | async-start | bytes 8388608
  273.9 22.4 %copy-start.13 = (bf16[2048,1280]{0,1:T(8,128)(2,1)S(1)}, bf16[2048,1280]{0,1:T(8,128)(2,1)}, u32[]{:S(2)}) copy-start(bf16[2048,1280]{0,1:T(8,128)(2,1)} %fusion.54) | copy-start | bytes 15728644
  296.3 23.8 %copy-start.10 = (f32[2048]{0:T(1024)S(1)}, f32[2048]{0:T(1024)}, u32[]{:S(2)}) copy-start(f32[2048]{0:T(1024)} %copy-done.9) | copy-start | bytes 24580
  332.5 22.8 %copy-start.12 = (f32[2048]{0:T(1024)S(1)}, f32[2048]{0:T(1024)}, u32[]{:S(2)}) copy-start(f32[2048]{0:T(1024)} %copy-done.11) | copy-start | bytes 24580
  411.3 11.2 %copy-start.4 = (bf16[2,80,256]{2,1,0:T(8,128)(2,1)S(1)}, bf16[2,80,256]{2,1,0:T(8,128)(2,1)}, u32[]{:S(2)}) copy-start(bf16[2,80,256]{2,1,0:T(8,128)(2,1)} %get-tuple-element.70) | copy-start | bytes 245764
  411.3 11.2 %copy-start.5 = (bf16[2,80,256]{2,1,0:T(8,128)(2,1)S(1)}, bf16[2,80,256]{2,1,0:T(8,128)(2,1)}, u32[]{:S(2)}) copy-start(bf16[2,80,256]{2,1,0:T(8,128)(2,1)} %get-tuple-element.71) | copy-start | bytes 245764
  411.3 11.2 %copy-start.6 = (bf16[2,80,256]{2,1,0:T(8,128)(2,1)S(1)}, bf16[2,80,256]{2,1,0:T(8,128)(2,1)}, u32[]{:S(2)}) copy-start(bf16[2,80,256]{2,1,0:T(8,128)(2,1)} %get-tuple-element.72) | copy-start | bytes 245764
  411.3 11.2 %copy-start.7 = (bf16[2,80,256]{2,1,0:T(8,128)(2,1)S(1)}, bf16[2,80,256]{2,1,0:T(8,128)(2,1)}, u32[]{:S(2)}) copy-start(bf16[2,80,256]{2,1,0:T(8,128)(2,1)} %get-tuple-element.73) | copy-start | bytes 245764
  411.3 11.2 %copy-start.8 = (bf16[2,80,256]{2,1,0:T(8,128)(2,1)S(1)}, bf16[2,80,256]{2,1,0:T(8,128)(2,1)}, u32[]{:S(2)}) copy-start(bf16[2,80,256]{2,1,0:T(8,128)(2,1)} %get-tuple-element.74) | copy-start | bytes 245764
  411.3 12.9 %copy-start.1 = (f32[2,20,3072]{2,0,1:T(2,128)S(1)}, f32[2,20,3072]{2,0,1:T(2,128)}, u32[]{:S(2)}) copy-start(f32[2,20,3072]{2,0,1:T(2,128)} %param.16) | copy-start | bytes 1474564
  422.4 207.9 %reduce-scatter.15.cloned.1.call-start = ((), (), s32[]{:S(2)}) async-start(), calls=%async_computation.7 | async-start | bytes 2088960
  839.3 22.5 %slice-start.4 = ((s8[15728640]{0:T(1024)(128)(4,1)}), s8[4194304]{0:T(1024)(128)(4,1)S(1)}, s32[]{:S(2)}) async-start(s8[15728640]{0:T(1024)(128)(4,1)} %bitcast.100), calls=%async_computation.12 | async-start | bytes 8388608
  845.8 15.9 %slice-start.5 = ((s8[15728640]{0:T(1024)(128)(4,1)}), s8[4194304]{0:T(1024)(128)(4,1)S(1)}, s32[]{:S(2)}) async-start(s8[15728640]{0:T(1024)(128)(4,1)} %bitcast.100), calls=%async_computation.13 | async-start | bytes 8388608
  845.8 15.9 %slice-start.6 = ((s8[15728640]{0:T(1024)(128)(4,1)}), s8[4194304]{0:T(1024)(128)(4,1)S(1)}, s32[]{:S(2)}) async-start(s8[15728640]{0:T(1024)(128)(4,1)} %bitcast.100), calls=%async_computation.14 | async-start | bytes 8388608
  845.8 15.9 %slice-start.7 = ((s8[15728640]{0:T(1024)(128)(4,1)}), s8[3145728]{0:T(1024)(128)(4,1)S(1)}, s32[]{:S(2)}) async-start(s8[15728640]{0:T(1024)(128)(4,1)} %bitcast.100), calls=%async_computation.15 | async-start | bytes 6291456
  845.8 23.9 %slice-start = ((s8[15728640]{0:T(1024)(128)(4,1)}), s8[4194304]{0:T(1024)(128)(4,1)S(1)}, s32[]{:S(2)}) async-start(s8[15728640]{0:T(1024)(128)(4,1)} %bitcast.97), calls=%async_computation.8 | async-start | bytes 8388608
  845.8 23.9 %slice-start.1 = ((s8[15728640]{0:T(1024)(128)(4,1)}), s8[4194304]{0:T(1024)(128)(4,1)S(1)}, s32[]{:S(2)}) async-start(s8[15728640]{0:T(1024)(128)(4,1)} %bitcast.97), calls=%async_computation.9 | async-start | bytes 8388608
  861.8 8.0 slice-start.2
  861.8 9.1 %slice-start.3 = ((s8[15728640]{0:T(1024)(128)(4,1)}), s8[3145728]{0:T(1024)(128)(4,1)S(1)}, s32[]{:S(2)}) async-start(s8[15728640]{0:T(1024)(128)(4,1)} %bitcast.97), calls=%async_computation.11 | async-start | bytes 6291456
  870.9 5.8 copy-start.3
  870.9 6.6 copy-start.2
Sparse Core Ops, SparseCore 0:
  217.3 79.3 reduce-scatter.10
  299.0 76.5 reduce-scatter.8
  422.6 79.1 reduce-scatter.12
  504.9 78.4 reduce-scatter.14
